TPU v7x, 32 devices: a whole 2x2x4 slice. The times are simulated.
32 devices in a mesh: tm: 4 (over y, x), space: 8 (over z, core).
Axes of the slice: x: 2, y: 2, z: 4, core: 2. Of those that a mesh axis runs over, the one named last changes fastest.
Arguments:
- states: float32 [4, 256, 256, 256], P('tm', 'space'), may hold values from -4 to 4
- forcing: float32 [4, 256, 256, 256], P('tm', 'space'), may hold values from -4 to 4
- inflow: float32 [256, 256, 256], P('space'), may hold values from -4 to 4
- timestep: float32 [1], replicated, may hold values from 0.05 to 0.2
Outputs:
- new_states: float32 [4, 256, 256, 256], P('tm', 'space')
- defects: float32 [4, 256, 256, 256], P('tm', 'space')
All inputs are finite; a program needn't handle non-finite values.
Results may differ from a plain program's by a relative error of at most 0.00013.
Values sent between devices are 32-bit elements; how exact they have to be, the bound alone decides.
No kernel may reach another device: no remote copies, remote signals or barrier semaphores. Data moves between devices by JAX's collectives and lax.ppermute only.
A program may use at most 192 MiB of HBM per device.

v0:
```python
import math

import jax
import jax.numpy as jnp
from jax import lax
from jax.sharding import PartitionSpec as P

FINE = 8


highest = lax.Precision.HIGHEST


def shifted(array, axis, by):
    length = lax.axis_size(axis)
    pairs = [(i, i + by) for i in range(length) if 0 <= i + by < length]
    return lax.ppermute(array, axis, pairs)


def prefix(part, axis, combine, identity):
    place = lax.axis_index(axis)
    gathered = jax.tree.map(lambda a: lax.all_gather(a, axis), part)
    state = jax.tree.map(lambda a, e: jnp.zeros_like(a) + jnp.asarray(e, a.dtype), part, identity)

    def one(lap, state):
        return combine(
            state, jax.tree.map(lambda a: lax.dynamic_index_in_dim(a, lap, 0, False), gathered)
        )

    return lax.fori_loop(0, place, one, state)


def hartley_table(extent):
    wavenumber = jnp.arange(extent, dtype=jnp.int32)
    product = wavenumber[:, None] * wavenumber[None, :] % extent
    angles = product.astype(jnp.float32) * (2.0 * math.pi / extent)
    return (jnp.cos(angles) + jnp.sin(angles)) * (1.0 / math.sqrt(extent))


def lattice_symbol(wavenumber, extent):
    angles = (wavenumber % extent).astype(jnp.float32) * (2.0 * math.pi / extent)
    return 2.0 - 2.0 * jnp.cos(angles)


def planar_forward(fields, hartley):
    rows_done = jnp.einsum("pzxy,ky->pzxk", fields, hartley, precision=highest)
    return jnp.einsum("pzxy,kx->pzky", rows_done, hartley, precision=highest)


def on_device(states, forcing, inflow, timestep):
    planes = states.shape[1]
    extent = states.shape[2]
    hartley = hartley_table(extent)
    stepsize = timestep[0]

    def depth_inverse(spectrum):
        return jnp.einsum("pkxy,kz->pzxy", spectrum, hartley, precision=highest)

    def width_inverse(blocks):
        return jnp.einsum("pzky,kx->pzxy", blocks, hartley, precision=highest)

    def planar_tail(blocks):
        return jnp.einsum("pzxk,ky->pzxy", blocks, hartley, precision=highest)

    stacked = jnp.concatenate([states, forcing, inflow[None]], axis=0)
    spectra = jnp.einsum(
        "pzxy,kz->pkxy",
        lax.all_to_all(
            planar_forward(stacked, hartley), "space", split_axis=2, concat_axis=1, tiled=True
        ),
        hartley,
        precision=highest,
    )
    spec_states = spectra[0:1]
    spec_forcing = spectra[1:2]
    spec_inflow = spectra[2:3]
    column = lax.axis_index("space") * planes + jnp.arange(planes, dtype=jnp.int32)
    full_symbol = lattice_symbol(jnp.arange(extent, dtype=jnp.int32), extent)
    local_symbol = lattice_symbol(column, extent)
    laplace = (
        lattice_symbol(jnp.arange(extent, dtype=jnp.int32), extent)[:, None, None]
        + local_symbol[None, :, None]
        + full_symbol[None, None, :]
    )
    damping = 1.0 / (1.0 + stepsize * laplace)
    propagator = jnp.ones_like(damping)
    accrued = jnp.zeros_like(damping)
    for repeat in range(FINE):
        propagator = propagator * damping
        accrued = accrued + propagator
    coarse = 1.0 / (1.0 + FINE * stepsize * laplace)
    propagator, source_gain, coarse = (propagator, stepsize * accrued, coarse)
    coarse_log = jnp.log(coarse)
    advanced = propagator * spec_states + source_gain * spec_forcing
    arrived = shifted(advanced, "tm", 1)
    opening = lax.axis_index("tm") == 0
    relaxed = jnp.where(opening, spec_inflow, arrived)
    defect_spec = propagator * (relaxed - spec_states)

    def compose(former, latter):
        return (former[0] + latter[0], jnp.exp(latter[0] * coarse_log) * former[1] + latter[1])

    single = jnp.ones((), jnp.float32)
    empty = (jnp.zeros((), jnp.float32), jnp.zeros_like(defect_spec))
    counted, correction = prefix((single, defect_spec), "tm", compose, empty)
    updated = relaxed + correction
    defect_field = width_inverse(
        lax.all_to_all(depth_inverse(defect_spec), "space", split_axis=1, concat_axis=2, tiled=True)
    )
    defect_out = planar_tail(defect_field)
    state_field = width_inverse(
        lax.all_to_all(depth_inverse(updated), "space", split_axis=1, concat_axis=2, tiled=True)
    )
    return (planar_tail(state_field), defect_out)


def solution(mesh):
    return jax.shard_map(
        on_device,
        mesh=mesh,
        in_specs=(
            P("tm", "space", None, None),
            P("tm", "space", None, None),
            P("space", None, None),
            P(),
        ),
        out_specs=(P("tm", "space", None, None), P("tm", "space", None, None)),
        check_vma=False,
    )
```

profile of v0, /device:TPU:6, one launch (start us, length us, event | category | flops | bytes accessed | tf_op | source)
XLA Modules:
  0.0 1498.1 jit_solution(14921202936366885212)
XLA Ops:
  8.2 26.0 %fusion.3 = f32[3,32,256,256]{3,2,1,0:T(8,128)} fusion(f32[1,32,256,256]{3,2,1,0:T(8,128)} %bitcast.113, f32[1,32,256,256]{3,2,1,0:T(8,128)} %param.7, f32[1,32,256,256]{3,2,1,0:T(8,128)} %param.6, f32[256,256,1,1]{1,0,3,2:T(8,128)S(1)} %fusion.127), kind=kOutput, calls=%fused_computation.5 | convolution fusion | flops 19339935744 | bytes 50593792 | tf_op jit(solution)/shard_map/pzxy,ky->pzxk/dot_general | solution.py:46
  34.3 33.0 %convolution_bitcast_fusion.1 = f32[3,32,256,256]{3,2,1,0:T(8,128)} fusion(f32[3,32,256,256]{3,2,1,0:T(8,128)} %fusion.3), kind=kOutput, calls=%fused_computation.22 | convolution fusion | flops 19328401408 | bytes 50331648 | tf_op jit(solution)/shard_map/pzxy,kx->pzky/dot_general | solution.py:47
  67.3 25.1 %copy.16 = f32[3,32,256,256]{3,1,0,2:T(8,128)} copy(f32[3,32,256,256]{3,2,1,0:T(8,128)} %convolution_bitcast_fusion.1) | data formatting | bytes 50331648 | tf_op jit(solution)/shard_map/pzxy,kx->pzky/transpose | solution.py:47
  99.8 542.4 %all-to-all-done = f32[3,32,256,256]{3,1,0,2:T(8,128)} async-done(((f32[3,32,256,256]{3,1,0,2:T(8,128)}), f32[3,32,256,256]{3,1,0,2:T(8,128)}, u32[]{:S(2)}, u32[]{:S(2)}) %all-to-all-start) | async-done | bytes 25165856 | tf_op jit(solution)/shard_map/all_to_all | solution.py:68
  642.2 17.8 %copy.17 = f32[3,32,8,32,256]{4,1,2,3,0:T(8,128)} copy(f32[3,32,8,32,256]{4,1,0,3,2:T(8,128)} %bitcast.7) | data formatting | bytes 50331648 | tf_op jit(solution)/shard_map/all_to_all | solution.py:68
  660.0 32.5 %convolution_bitcast_fusion = f32[3,256,32,256]{3,1,2,0:T(8,128)} fusion(f32[3,256,32,256]{3,1,2,0:T(8,128)} %bitcast.109), kind=kOutput, calls=%fused_computation.21 | convolution fusion | flops 19328401408 | bytes 50331648 | tf_op jit(solution)/shard_map/pzxy,kz->pkxy/dot_general | solution.py:66
  692.5 12.0 fusion.22
  705.8 182.8 %collective-permute-done = f32[1,256,32,256]{3,1,2,0:T(8,128)} collective-permute-done((f32[1,256,32,256]{3,1,2,0:T(8,128)}, f32[1,256,32,256]{3,1,2,0:T(8,128)}, u32[]{:S(2)}, u32[]{:S(2)}) %collective-permute-start) | collective-permute-done | bytes 8388640 | tf_op jit(solution)/shard_map/ppermute | solution.py:17
  888.6 10.0 subtract_multiply_fusion
  910.3 13.1 fusion.34
  923.4 10.1 copy.27
  940.0 8.9 all-reduce
  948.9 257.1 %all-gather.3.cloned.1.call-done = f32[4,256,32,256]{3,2,1,0:T(8,128)} async-done(((f32[1,256,32,256]{3,2,1,0:T(8,128)}), f32[4,256,32,256]{3,2,1,0:T(8,128)}) %all-gather.3.cloned.1.call-update) | async-done | bytes 33554448 | tf_op jit(solution)/shard_map/all_gather | solution.py:22
  1210.5 37.8 %while.13 = (s32[]{:T(128)}, f32[1,256,32,256]{3,2,1,0:T(8,128)}, s32[]{:T(128)}, f32[4]{0:T(128)S(1)}, f32[4,1,256,32,256]{4,3,2,1,0:T(8,128)}, /*index=5*/f32[...) while((s32[]{:T(128)}, f32[1,256,32,256]{3,2,1,0:T(8,128)}, ...), condition=%wide.region_1.2_spmd.clone, body=%wide.region_0.1_spmd.clone.sunk | while | flops 14680069 | bytes 25199792 | solution.py:30
  1211.1 12.0 bitcast_add_fusion.2
  1223.7 12.0 bitcast_add_fusion.2
  1236.3 12.0 bitcast_add_fusion.2
  1248.3 20.1 %fusion.31 = f32[1,256,32,256]{3,1,2,0:T(8,128)S(1)} fusion(f32[1,256,32,256]{3,2,1,0:T(8,128)} %get-tuple-element.53, f32[1,256,32,256]{3,1,2,0:T(8,128)} %collective-permute-done, f32[3,256,32,256]{3,1,2,0:T(8,128)} %convolution_bitcast_fusion, pred[]{:T(512)S(6)} %eq.10), kind=kOutput, calls=%fused_computation.41 | convolution fusion | flops 6447693824 | bytes 33554432 | tf_op jit(solution)/shard_map/pkxy,kz->pzxy/dot_general | solution.py:57
  1268.4 8.3 copy.23
  1286.2 9.7 fusion.50
  1295.9 21.5 %fusion.40 = f32[1,32,256,256]{3,2,1,0:T(8,128)} fusion(f32[256,32,256]{2,0,1:T(8,128)S(1)} %fusion.50), kind=kOutput, calls=%fused_computation.44 | convolution fusion | flops 6443499520 | bytes 16777216 | tf_op jit(solution)/shard_map/pzxk,ky->pzxy/dot_general | solution.py:63
  1317.5 148.3 %all-to-all-done.1 = f32[1,256,32,256]{3,2,0,1:T(8,128)} async-done(((f32[1,256,32,256]{3,2,0,1:T(8,128)}), f32[1,256,32,256]{3,2,0,1:T(8,128)}, u32[]{:S(2)}, u32[]{:S(2)}) %all-to-all-start.1) | async-done | bytes 8388640 | tf_op jit(solution)/shard_map/all_to_all | solution.py:112
  1470.1 9.7 fusion.55
  1479.8 11.2 fusion.37
  (26 shorter events, 47.2 us)
Async XLA Ops:
  92.4 549.8 %all-to-all-start = ((f32[3,32,256,256]{3,1,0,2:T(8,128)}), f32[3,32,256,256]{3,1,0,2:T(8,128)}, u32[]{:S(2)}, u32[]{:S(2)}) async-start(f32[3,32,256,256]{3,1,0,2:T(8,128)} %copy.16), calls=%async_computation | async-start | bytes 50331648 | tf_op jit(solution)/shard_map/all_to_all | solution.py:68
  98.8 1107.2 %all-gather.3.cloned.1.call-start = ((), (), s32[]{:S(2)}) async-start(), calls=%async_computation.3 | async-start | bytes 41943040 | tf_op jit(solution)/shard_map/all_gather | solution.py:22
  704.5 184.1 %collective-permute-start = (f32[1,256,32,256]{3,1,2,0:T(8,128)}, f32[1,256,32,256]{3,1,2,0:T(8,128)}, u32[]{:S(2)}, u32[]{:S(2)}) collective-permute-start(f32[1,256,32,256]{3,1,2,0:T(8,128)} %fusion.22), channel_id=1, source_target_pairs={{0,8},{8,16},{16,24},{1,9},{9,17},{17,25},{2,10},{10,18},{18,26},{... | collective-permute-start | bytes 25165832 | tf_op jit(solution)/shard_map/ppermute | solution.py:17
  898.6 3.4 copy-start
  933.6 5.1 copy-start.1
  933.6 343.1 %all-to-all-start.2 = ((f32[1,256,32,256]{3,2,0,1:T(8,128)}), f32[1,256,32,256]{3,2,0,1:T(8,128)}, u32[]{:S(2)}, u32[]{:S(2)}) async-start(f32[1,256,32,256]{3,2,0,1:T(8,128)} %copy.27), calls=%async_computation.2 | async-start | bytes 16777216 | tf_op jit(solution)/shard_map/all_to_all | solution.py:108
  1276.7 189.1 %all-to-all-start.1 = ((f32[1,256,32,256]{3,2,0,1:T(8,128)}), f32[1,256,32,256]{3,2,0,1:T(8,128)}, u32[]{:S(2)}, u32[]{:S(2)}) async-start(f32[1,256,32,256]{3,2,0,1:T(8,128)} %copy.23), calls=%async_computation.1 | async-start | bytes 16777216 | tf_op jit(solution)/shard_map/all_to_all | solution.py:112
Sparse Core Ops, SparseCore 0:
  910.4 295.6 all-gather.2
where the time goes:
time: 1500 us
  waiting for transfers between devices  1130 us (75%)
  matrix products  177 us (12%)
  local copies, waits for them, and re-layouts  89.1 us (6%)
  other arithmetic  59.2 us (4%)
  starting transfers between devices  18 us (1%)
  between operations  15.1 us (1%)
    all_to_all x1, waiting for transfers between devices, on_device(): lax.all_to_all(planar_forward(stacked, hartley), 'space', split_axis=2, c...  542 us
    all_gather x1, waiting for transfers between devices, prefix(): gathered = jax.tree.map(lambda a: lax.all_gather(a, axis), part)  257 us
    ppermute x1, waiting for transfers between devices, shifted(): return lax.ppermute(array, axis, pairs)  183 us
    all_to_all x1, waiting for transfers between devices, on_device(): lax.all_to_all(depth_inverse(updated), 'space', split_axis=1, concat_axis...  148 us
    add x3, other arithmetic, compose(): jnp.exp(latter[0] * coarse_log) * former[1] + latter[1]  36 us
    dot_general x2, matrix products, depth_inverse(): return jnp.einsum('pkxy,kz->pzxy', spectrum, hartley, precision=highest)  33.2 us
    dot_general x1, matrix products, planar_forward(): return jnp.einsum('pzxy,kx->pzky', rows_done, hartley, precision=highest)  33 us
    dot_general x2, matrix products, planar_tail(): return jnp.einsum('pzxk,ky->pzxy', blocks, hartley, precision=highest)  32.8 us
  transfers between devices with their start and end apart: 5, of which 4 were waited for; matrix products, arithmetic and copies ran while one was open for 9% of the time, Pallas kernels for 0%

commit v1 on v0

v1 whole, which is shorter than its diff:
```python
import math

import jax
import jax.numpy as jnp
from jax import lax
from jax.experimental import pallas as pl
from jax.experimental.pallas import tpu as pltpu
from jax.sharding import Mesh, PartitionSpec as P

FINE = 8
CHUNKS = 4
SUB = 8
LANE = 128
VMEM = 56 * 1024 * 1024


def hartley_table(extent):
    wavenumber = jnp.arange(extent, dtype=jnp.int32)
    product = wavenumber[:, None] * wavenumber[None, :] % extent
    angles = product.astype(jnp.float32) * (2.0 * math.pi / extent)
    return (jnp.cos(angles) + jnp.sin(angles)) * (1.0 / math.sqrt(extent))


def lattice_symbol(wavenumber, extent):
    angles = (wavenumber % extent).astype(jnp.float32) * (2.0 * math.pi / extent)
    return 2.0 - 2.0 * jnp.cos(angles)


def power(base, exponent):
    result = None
    while exponent:
        if exponent & 1:
            result = base if result is None else result * base
        exponent >>= 1
        if exponent:
            base = base * base
    return result


def filter_of(mu, step, order):
    r = 2.0 + mu + 1.0 / step
    z = 2.0 / (r + jnp.sqrt(r * r - 4.0))
    inverse = 1.0 / (1.0 - z * z)
    lead = z / step * inverse
    base = [lead]
    term = lead * (z * z * inverse)
    for _ in range(order - 1):
        base.append(term)
        term = term * inverse
    current = base
    weights = []
    for j in range(1, order + 1):
        if j > 1:
            current = [
                sum((current[i] * base[k - i] for i in range(1, k + 1)), current[0] * base[k])
                for k in range(order)
            ]
        weights.append([current[j - m] for m in range(1, j + 1)])
    return z, weights


def coef_count(intervals):
    rounds = intervals - 2
    return 3 + 2 * FINE + 2 + 3 + rounds * (rounds + 1) // 2 + rounds


def coef_kernel(step_ref, mu_ref, out_ref, *, block, extent, intervals):
    step = step_ref[0]
    mu = mu_ref[...]
    rounds = intervals - 2
    step_v = jnp.zeros_like(mu) + step
    z, weights = filter_of(mu, step_v, FINE)
    prop = weights[FINE - 1]
    gain = [
        step_v * sum((weights[j - 1][m - 1] for j in range(m + 1, FINE + 1)), weights[m - 1][m - 1])
        for m in range(1, FINE + 1)
    ]
    rows = [z, power(z, block), power(z, extent)] + prop + gain
    rows += [sum(prop[1:], prop[0]), sum(gain[1:], gain[0])]
    z, weights = filter_of(mu, FINE * step_v, rounds)
    rows += [z, power(z, block), power(z, extent)]
    for one in weights:
        rows += one
    for one in weights:
        rows.append(sum(one[1:], one[0]))
    for i, row in enumerate(rows):
        out_ref[i] = row


class Coefs:
    def __init__(self, ref, intervals):
        rounds = intervals - 2
        self.z, self.zn, self.zl = ref[0], ref[1], ref[2]
        at = 3
        self.prop = lambda m: ref[2 + m]
        self.gain = lambda m: ref[2 + FINE + m]
        at += 2 * FINE
        self.prop0 = lambda: ref[at]
        self.gain0 = lambda: ref[at + 1]
        at2 = at + 2
        self.coarse_z = lambda: (ref[at2], ref[at2 + 1], ref[at2 + 2])
        at3 = at2 + 3
        self.coarse = lambda j, m: ref[at3 + (j - 1) * j // 2 + m - 1]
        at4 = at3 + rounds * (rounds + 1) // 2
        self.coarse0 = lambda j: ref[at4 + j - 1]


def inflow_state(blocks, zn, zl, block, extent):
    order = len(blocks[0])

    def carried(state, factor, length):
        return [
            factor
            * sum(
                (math.comb(length + i - 1, i) * 1.0 * state[m + i] for i in range(1, order - m)),
                state[m],
            )
            for m in range(order)
        ]

    state = blocks[-1]
    for nearer in blocks[-2::-1]:
        state = [a + b for a, b in zip(nearer, carried(state, zn, block))]
    solved = [None] * order
    closure = 1.0 / (1.0 - zl)
    for m in reversed(range(order)):
        total = state[m]
        for i in range(1, order - m):
            total = total + zl * (math.comb(extent + i - 1, i) * 1.0) * solved[m + i]
        solved[m] = total * closure
    return solved


def sweep(count, body, init, unroll=8):
    unroll = min(unroll, count)

    def group(g, carry):
        for k in range(unroll):
            carry = body(g * unroll + k, carry)
        return carry

    return lax.fori_loop(0, count // unroll, group, init)


def cascade(z, x, states):
    out = []
    for y in states:
        x = z * y + x
        out.append(x)
    return out


def nested(z, inputs, states):
    out = [None] * len(states)
    above = None
    for m in reversed(range(len(states))):
        x = inputs[m] if above is None else inputs[m] + above
        above = z * states[m] + x
        out[m] = above
    return out


def advance_ends_kernel(coef_ref, s_ref, f_ref, out_ref, *, block, extent, intervals):
    c = Coefs(coef_ref, intervals)
    z = c.z
    zero = [jnp.zeros_like(z)] * FINE
    for side in range(2):

        def one(i, carry):
            n = i if side == 0 else block - 1 - i
            return (
                cascade(z, s_ref[0, n], carry[0]),
                cascade(z, f_ref[0, n], carry[1]),
            )

        ys, yf = sweep(block, one, (zero, zero))
        for m in range(FINE):
            out_ref[side, 0, m] = sum(
                (
                    c.prop(m + i + 1) * ys[i] + c.gain(m + i + 1) * yf[i]
                    for i in range(1, FINE - m)
                ),
                c.prop(m + 1) * ys[0] + c.gain(m + 1) * yf[0],
            )


def upstream(place, count, side, d):
    return lax.rem(place + (count - d if side == 0 else d), count)


def ends_of(c, x_ref, out_ref, block):
    z = c.z
    zero = [jnp.zeros_like(z)] * FINE
    for side in range(2):

        def one(i, carry):
            n = i if side == 0 else block - 1 - i
            return cascade(z, x_ref[0, n], carry)

        y = sweep(block, one, zero)
        for m in range(FINE):
            out_ref[side, 0, m] = sum(
                (c.prop(m + i + 1) * y[i] for i in range(1, FINE - m)), c.prop(m + 1) * y[0]
            )


def relax_kernel(
    place_ref, coef_ref, s_ref, f_ref, own_ref, ends_ref, rel_ref, err_ref, out_ref, *, block, extent, intervals
):
    c = Coefs(coef_ref, intervals)
    z = c.z
    count = extent // block
    place = place_ref[0]
    t = pl.program_id(2)

    @pl.when(t == 0)
    def _():
        def one(n, carry):
            value = f_ref[0, n]
            rel_ref[0, n] = value
            err_ref[0, n] = value - own_ref[0, n]
            return carry

        sweep(block, one, 0)

    @pl.when(t > 0)
    def _():
        prop = [c.prop(m + 1) for m in range(FINE)]
        gain = [c.gain(m + 1) for m in range(FINE)]
        for side in range(2):
            start = inflow_state(
                [
                    [ends_ref[upstream(place, count, side, d), side, 0, m] for m in range(FINE)]
                    for d in range(1, count + 1)
                ],
                c.zn,
                c.zl,
                block,
                extent,
            )
            if side == 0:
                prop0, gain0 = c.prop0(), c.gain0()

            def one(i, carry):
                n = i if side == 0 else block - 1 - i
                s = s_ref[0, n]
                f = f_ref[0, n]
                carry = nested(z, [p * s + g * f for p, g in zip(prop, gain)], carry)
                if side == 0:
                    rel_ref[0, n] = carry[0] - (prop0 * s + gain0 * f)
                else:
                    value = rel_ref[0, n] + carry[0]
                    rel_ref[0, n] = value
                    err_ref[0, n] = value - own_ref[0, n]
                return carry

            sweep(block, one, start)

    ends_of(c, err_ref, out_ref, block)


def coarse_inputs(c, d, j):
    return [
        sum(
            (c.coarse(j - 1 - i, m) * d[i] for i in range(1, j - m)),
            c.coarse(j - 1, m) * d[0],
        )
        for m in range(1, j)
    ]


def defect_kernel(
    place_ref, coef_ref, err_ref, ends_ref, def_ref, out_ref, *, block, extent, intervals
):
    c = Coefs(coef_ref, intervals)
    z = c.z
    count = extent // block
    place = place_ref[0]

    def interval(t, carry):
        prop = [c.prop(m + 1) for m in range(FINE)]
        for side in range(2):
            start = inflow_state(
                [
                    [ends_ref[upstream(place, count, side, d), side, t, m] for m in range(FINE)]
                    for d in range(1, count + 1)
                ],
                c.zn,
                c.zl,
                block,
                extent,
            )
            if side == 0:
                prop0 = c.prop0()

            def one(i, carry):
                n = i if side == 0 else block - 1 - i
                x = err_ref[t, n]
                carry = nested(z, [p * x for p in prop], carry)
                if side == 0:
                    def_ref[t, n] = carry[0] - prop0 * x
                else:
                    def_ref[t, n] = def_ref[t, n] + carry[0]
                return carry

            sweep(block, one, start)
        return carry

    lax.fori_loop(0, intervals, interval, 0)
    cz, _, _ = c.coarse_z()
    sizes = [j - 1 for j in range(2, intervals)]
    for side in range(2):

        def one(i, carry):
            n = i if side == 0 else block - 1 - i
            d = [def_ref[t, n] for t in range(intervals - 2)]
            return [
                nested(cz, coarse_inputs(c, d, j), state)
                for j, state in zip(range(2, intervals), carry)
            ]

        ends = sweep(block, one, [[jnp.zeros_like(cz)] * k for k in sizes])
        at = 0
        for state in ends:
            for value in state:
                out_ref[side, at] = value
                at += 1


def correct_kernel(
    place_ref, coef_ref, rel_ref, def_ref, ends_ref, new_ref, *, block, extent, intervals
):
    c = Coefs(coef_ref, intervals)
    count = extent // block
    place = place_ref[0]
    cz, czn, czl = c.coarse_z()
    for side in range(2):
        starts = []
        at = 0
        for j in range(2, intervals):
            starts.append(
                inflow_state(
                    [
                        [ends_ref[upstream(place, count, side, d), side, at + m] for m in range(j - 1)]
                        for d in range(1, count + 1)
                    ],
                    czn,
                    czl,
                    block,
                    extent,
                )
            )
            at += j - 1

        def one(i, carry):
            n = i if side == 0 else block - 1 - i
            d = [def_ref[t, n] for t in range(intervals - 1)]
            carry = [
                nested(cz, coarse_inputs(c, d, j), state)
                for j, state in zip(range(2, intervals), carry)
            ]
            if side == 0:
                new_ref[0, n] = rel_ref[0, n]
                new_ref[1, n] = rel_ref[1, n] + d[0]
            for j, state in zip(range(2, intervals), carry):
                if side == 0:
                    center = sum(
                        (c.coarse0(j - 1 - i) * d[i] for i in range(1, j - 1)),
                        c.coarse0(j - 1) * d[0],
                    )
                    new_ref[j, n] = rel_ref[j, n] + d[j - 1] + (state[0] - center)
                else:
                    new_ref[j, n] = new_ref[j, n] + state[0]
            return carry

        sweep(block, one, starts, 4)


def split(x):
    high = x.astype(jnp.bfloat16)
    return high, (x - high.astype(jnp.float32)).astype(jnp.bfloat16)


def dot3(a, b):
    def dot(x, y):
        return jnp.dot(x, y, preferred_element_type=jnp.float32)

    return dot(a[0], b[0]) + (dot(a[0], b[1]) + dot(a[1], b[0]))


def forward_kernel(*refs, choose, chunks):
    if choose:
        last_ref, x_ref, other_ref, high_ref, low_ref = refs[:5]
        outs = refs[5:]
    else:
        x_ref, high_ref, low_ref = refs[:3]
        outs = refs[3:]
    table = (high_ref[...], low_ref[...])
    planes = x_ref.shape[0]
    for p in range(planes):
        x = x_ref[p]
        if choose:
            x = jnp.where(last_ref[0] > 0, other_ref[p], x)
        y = dot3(table, split(dot3(split(x), table)))
        groups, rows = outs[0].shape[0], outs[0].shape[2]
        y = y.reshape(groups, chunks * rows, y.shape[-1])
        for i, out in enumerate(outs):
            out[:, p] = y[:, i * rows : (i + 1) * rows]


def inverse_kernel(*refs):
    parts, (high_ref, low_ref, out_ref) = refs[:-3], refs[-3:]
    table = (high_ref[...], low_ref[...])
    extent = out_ref.shape[-1]
    for p in range(out_ref.shape[0]):
        x = jnp.concatenate([part[:, p] for part in parts], axis=1).reshape(extent, extent)
        out_ref[p] = dot3(split(dot3(table, split(x))), table)


def on_device(states, forcing, inflow, timestep):
    planes, extent = states.shape[1], states.shape[2]
    intervals = lax.axis_size("tm")
    cores = lax.axis_size("core")
    count = lax.axis_size("line")
    block = planes * cores
    groups = intervals * cores
    rows = extent // groups
    chunks = max(1, min(CHUNKS, rows // SUB))
    part = rows // chunks
    f32 = jnp.float32
    params = lambda n: pltpu.CompilerParams(
        dimension_semantics=("arbitrary",) * n, vmem_limit_bytes=VMEM
    )
    sizes = dict(block=block, extent=extent, intervals=intervals)

    hartley = hartley_table(extent)
    high = lax.reduce_precision(hartley, 8, 7)
    tables = (high.astype(jnp.bfloat16), (hartley - high).astype(jnp.bfloat16))

    step = 4
    table_spec = pl.BlockSpec((extent, extent), lambda a: (0, 0))
    plane_spec = pl.BlockSpec((step, extent, extent), lambda a: (a, 0, 0))
    part_spec = pl.BlockSpec((groups, step, part, extent), lambda a: (0, a, 0, 0))
    part_shape = jax.ShapeDtypeStruct((groups, planes, part, extent), f32)

    def forward(field, other=None):
        choose = other is not None
        last = (lax.axis_index("tm") == intervals - 1).astype(jnp.int32).reshape(1)
        extra = [pl.BlockSpec(memory_space=pltpu.SMEM)] if choose else []
        return pl.pallas_call(
            lambda *r: forward_kernel(*r, choose=choose, chunks=chunks),
            grid=(planes // step,),
            in_specs=extra + [plane_spec] * (1 + choose) + [table_spec] * 2,
            out_specs=[part_spec] * chunks,
            out_shape=[part_shape] * chunks,
            compiler_params=params(1),
            name="forward",
        )(*([last] if choose else []), field, *([other] if choose else []), *tables)

    def inverse(parts):
        return pl.pallas_call(
            inverse_kernel,
            grid=(planes // step,),
            in_specs=[part_spec] * chunks + [table_spec] * 2,
            out_specs=plane_spec,
            out_shape=jax.ShapeDtypeStruct((planes, extent, extent), f32),
            compiler_params=params(1),
            name="inverse",
        )(*parts, *tables)

    def exchange(x):
        return lax.all_to_all(x, ("tm", "core"), split_axis=0, concat_axis=0, tiled=True)

    def line_gather(x):
        return lax.all_gather(x, "line", axis=0)

    sent_states = forward(states[0])
    sent_sources = forward(forcing[0], inflow)

    group = lax.axis_index("tm") * cores + lax.axis_index("core")
    place = lax.axis_index("line").astype(jnp.int32).reshape(1)
    wavenumber = group * rows + jnp.arange(rows, dtype=jnp.int32)
    mu = (
        lattice_symbol(wavenumber, extent)[:, None]
        + lattice_symbol(jnp.arange(extent, dtype=jnp.int32), extent)[None, :]
    )
    ncoef = coef_count(intervals)
    coefs = pl.pallas_call(
        lambda *r: coef_kernel(*r, **sizes),
        grid=(rows // SUB, extent // LANE),
        in_specs=[
            pl.BlockSpec(memory_space=pltpu.SMEM),
            pl.BlockSpec((SUB, LANE), lambda r, l: (r, l)),
        ],
        out_specs=pl.BlockSpec((ncoef, SUB, LANE), lambda r, l: (0, r, l)),
        out_shape=jax.ShapeDtypeStruct((ncoef, rows, extent), f32),
        compiler_params=params(2),
        name="coefs",
    )(timestep, mu)

    grid2 = (part // SUB, extent // LANE)
    whole = (intervals, block, part, extent)
    smem = pl.BlockSpec(memory_space=pltpu.SMEM)

    def one_spec(pick):
        return pl.BlockSpec((1, block, SUB, LANE), lambda r, l, t: (pick(t), 0, r, l))

    all_spec = pl.BlockSpec((intervals, block, SUB, LANE), lambda r, l: (0, 0, r, l))
    before = lambda t: lax.rem(t + intervals - 1, intervals)
    same = lambda t: t
    ncoarse = (intervals - 1) * (intervals - 2) // 2

    defect_parts = []
    state_parts = []
    for i in range(chunks):
        first = i * part // SUB
        coef3 = pl.BlockSpec((ncoef, SUB, LANE), lambda r, l, t: (0, first + r, l))
        coef2 = pl.BlockSpec((ncoef, SUB, LANE), lambda r, l: (0, first + r, l))
        s = exchange(sent_states[i]).reshape(whole)
        f = exchange(sent_sources[i]).reshape(whole)
        ends = pl.pallas_call(
            lambda *r: advance_ends_kernel(*r, **sizes),
            grid=grid2 + (intervals - 1,),
            in_specs=[coef3, one_spec(same), one_spec(same)],
            out_specs=pl.BlockSpec((2, 1, FINE, SUB, LANE), lambda r, l, t: (0, t, 0, r, l)),
            out_shape=jax.ShapeDtypeStruct((2, intervals - 1, FINE, part, extent), f32),
            compiler_params=params(3),
            name="advance_ends",
        )(coefs, s, f)
        ends = line_gather(ends)
        relaxed, error, ends = pl.pallas_call(
            lambda *r: relax_kernel(*r, **sizes),
            grid=grid2 + (intervals,),
            in_specs=[
                smem,
                coef3,
                one_spec(before),
                one_spec(before),
                one_spec(same),
                pl.BlockSpec(
                    (count, 2, 1, FINE, SUB, LANE),
                    lambda r, l, t: (0, 0, jnp.maximum(t - 1, 0), 0, r, l),
                ),
            ],
            out_specs=[
                one_spec(same),
                one_spec(same),
                pl.BlockSpec((2, 1, FINE, SUB, LANE), lambda r, l, t: (0, t, 0, r, l)),
            ],
            out_shape=[
                jax.ShapeDtypeStruct(whole, f32),
                jax.ShapeDtypeStruct(whole, f32),
                jax.ShapeDtypeStruct((2, intervals, FINE, part, extent), f32),
            ],
            compiler_params=params(3),
            name="relax",
        )(place, coefs, s, f, s, ends)
        ends = line_gather(ends)
        defect, ends = pl.pallas_call(
            lambda *r: defect_kernel(*r, **sizes),
            grid=grid2,
            in_specs=[
                smem,
                coef2,
                all_spec,
                pl.BlockSpec(
                    (count, 2, intervals, FINE, SUB, LANE), lambda r, l: (0, 0, 0, 0, r, l)
                ),
            ],
            out_specs=[
                all_spec,
                pl.BlockSpec((2, ncoarse, SUB, LANE), lambda r, l: (0, 0, r, l)),
            ],
            out_shape=[
                jax.ShapeDtypeStruct(whole, f32),
                jax.ShapeDtypeStruct((2, ncoarse, part, extent), f32),
            ],
            compiler_params=params(2),
            name="defect",
        )(place, coefs, error, ends)
        defect_parts.append(exchange(defect.reshape(part_shape.shape)))
        ends = line_gather(ends)
        updated = pl.pallas_call(
            lambda *r: correct_kernel(*r, **sizes),
            grid=grid2,
            in_specs=[
                smem,
                coef2,
                all_spec,
                all_spec,
                pl.BlockSpec((count, 2, ncoarse, SUB, LANE), lambda r, l: (0, 0, 0, r, l)),
            ],
            out_specs=all_spec,
            out_shape=jax.ShapeDtypeStruct(whole, f32),
            compiler_params=params(2),
            name="correct",
        )(place, coefs, relaxed, defect, ends)
        state_parts.append(exchange(updated.reshape(part_shape.shape)))
    return inverse(state_parts)[None], inverse(defect_parts)[None]


def solution(mesh):
    intervals, spaces = mesh.shape["tm"], mesh.shape["space"]
    cores = 2
    inner = Mesh(
        mesh.devices.reshape(intervals, spaces // cores, cores), ("tm", "line", "core")
    )
    field = P("tm", ("line", "core"), None, None)
    return jax.shard_map(
        on_device,
        mesh=inner,
        in_specs=(field, field, P(("line", "core"), None, None), P()),
        out_specs=(field, field),
        check_vma=False,
    )
```

time: 1500 us -> 687 us (0.46)
  waiting for transfers between devices: 1130 us -> 106 us
  blocking collectives: 8.93 us -> 307 us
  Pallas kernels: 0 us -> 204 us
  matrix products: 177 us -> 0 us
  local copies, waits for them, and re-layouts: 89.1 us -> 4.13 us
  other arithmetic: 59.2 us -> 2.57 us
  starting transfers between devices: 18 us -> 42.5 us
    all_to_all x3 -> x8, waiting for transfers between devices: 691 us -> 58.2 us  [exchange(): lax.all_to_all(x, ('tm', 'core'), split_axis=0, concat_axis=0, tiled=True)]
    all_to_all x0 -> x8, blocking collectives: none -> 241 us  [exchange(): lax.all_to_all(x, ('tm', 'core'), split_axis=0, concat_axis=0, tiled=True)]
    all_gather x1 -> x8, waiting for transfers between devices: 257 us -> 47.2 us  [line_gather(): return lax.all_gather(x, 'line', axis=0)]
    pallas_call x0 -> x21, Pallas kernels: none -> 204 us  [the longest x4 58.3 us: on_device(): pl.pallas_call(lambda *r: relax_kernel(*r, **sizes), grid=grid2 + (interv...]
    ppermute x1 -> x0, waiting for transfers between devices: 183 us -> none  [shifted(): return lax.ppermute(array, axis, pairs)]
    dot_general x9 -> x0, matrix products: 177 us -> none  [the longest x2 33.2 us: depth_inverse(): return jnp.einsum('pkxy,kz->pzxy', spectrum, hartley, precision=highest)]
    all_gather x0 -> x4, blocking collectives: none -> 65.2 us  [line_gather(): return lax.all_gather(x, 'line', axis=0)]
    add x5 -> x1, other arithmetic: 48.1 us -> 0.69 us  [on_device(): lattice_symbol(wavenumber, extent)[:, None]]
  transfers between devices with their start and end apart: 5 -> 16, of which waited for: 4 -> 8; matrix products, arithmetic and copies ran while one was open for 9% -> 0% of each run, Pallas kernels for 0% -> 26%
where the time goes in v1:
time: 687 us; the launch traced here: 681 us
  blocking collectives  307 us (45%)
  Pallas kernels  204 us (30%)
  waiting for transfers between devices  106 us (15%)
  starting transfers between devices  42.5 us (6%)
  between operations  14.8 us (2%)
    all_to_all x8, blocking collectives, exchange(): lax.all_to_all(x, ('tm', 'core'), split_axis=0, concat_axis=0, tiled=True)  241 us
    all_gather x4, blocking collectives, line_gather(): return lax.all_gather(x, 'line', axis=0)  65.2 us
    pallas_call x4, Pallas kernels, on_device(): pl.pallas_call(lambda *r: relax_kernel(*r, **sizes), grid=grid2 + (interv...  58.3 us
    all_to_all x8, waiting for transfers between devices, exchange(): lax.all_to_all(x, ('tm', 'core'), split_axis=0, concat_axis=0, tiled=True)  58.2 us
    all_gather x8, waiting for transfers between devices, line_gather(): return lax.all_gather(x, 'line', axis=0)  47.2 us
    pallas_call x4, Pallas kernels, on_device(): pl.pallas_call(lambda *r: defect_kernel(*r, **sizes), grid=grid2, in_spec...  42.3 us
    all_to_all x8, starting transfers between devices, exchange(): lax.all_to_all(x, ('tm', 'core'), split_axis=0, concat_axis=0, tiled=True)  42.3 us
    pallas_call x2, Pallas kernels, forward(): pl.pallas_call(lambda *r: forward_kernel(*r, choose=choose, chunks=chunks...  28.9 us
  transfers between devices with their start and end apart: 16, of which 8 were waited for; matrix products, arithmetic and copies ran while one was open for 0% of the time, Pallas kernels for 26%

profile of v1, /device:TPU:6, one launch (start us, length us, event | category | flops | bytes accessed | tf_op | source)
XLA Modules:
  0.0 680.6 jit_solution(8548324937154381944)
XLA Ops:
  8.9 13.7 %forward.2 = (f32[8,32,8,256]{3,2,1,0:T(8,128)}, f32[8,32,8,256]{3,2,1,0:T(8,128)}, f32[8,32,8,256]{3,2,1,0:T(8,128)}, f32[8,32,8,256]{3,2,1,0:T(8,128)}) custom-call(f32[32,256,256]{2,1,0:T(8,128)} %bitcast.55, bf16[256,256]{1,0:T(8,128)(2,1)} %get-tuple-element.58.r_1_.r_3_.refs_4_, bf16[256,256]{1,0:T(8,128)(2,1)} %get-tuple-element.59.r_2_.r_4_.refs_5_), custom_call_target="tpu_custom_call" | custom-call | tf_op jit(solution)/shard_map/forward/pallas_call | solution.py:450
  26.9 15.2 %forward.3 = (f32[8,32,8,256]{3,2,1,0:T(8,128)}, f32[8,32,8,256]{3,2,1,0:T(8,128)}, f32[8,32,8,256]{3,2,1,0:T(8,128)}, f32[8,32,8,256]{3,2,1,0:T(8,128)}) custom-call(s32[1]{0:T(128)} %bitcast.3.r_0_, f32[32,256,256]{2,1,0:T(8,128)} %bitcast.54, f32[32,256,256]{2,1,0:T(8,128)} %r_2_.1, bf16[256,256]{1,0:T(8,128)(2,1)} %get-tuple-element.58.r_1_.r_3_.refs_4_, ...), custom_call_target="tpu_custom_call" | custom-call | tf_op jit(solution)/shard_map/forward/pallas_call | solution.py:450
  51.2 31.1 %all_to_all.80 = f32[8,32,8,256]{3,2,1,0:T(8,128)} all-to-all(f32[8,32,8,256]{3,2,1,0:T(8,128)} %get-tuple-element.31), channel_id=1, replica_groups=mesh['tm'=4,'line'=4,'core'=2] {'tm','core'}, dimensions={0} | all-to-all | bytes 4194304 | tf_op jit(solution)/shard_map/all_to_all | solution.py:472
  82.3 29.7 %all_to_all.81 = f32[8,32,8,256]{3,2,1,0:T(8,128)} all-to-all(f32[8,32,8,256]{3,2,1,0:T(8,128)S(1)} %copy-done.10), channel_id=1, replica_groups=mesh['tm'=4,'line'=4,'core'=2] {'tm','core'}, dimensions={0} | all-to-all | bytes 4194304 | tf_op jit(solution)/shard_map/all_to_all | solution.py:472
  130.9 11.3 %all-to-all-done.4 = f32[8,32,8,256]{3,2,1,0:T(8,128)S(1)} async-done(((f32[8,32,8,256]{3,2,1,0:T(8,128)}), f32[8,32,8,256]{3,2,1,0:T(8,128)S(1)}, u32[]{:S(2)}, u32[]{:S(2)}) %all-to-all-start.4) | async-done | bytes 2097184 | tf_op jit(solution)/shard_map/all_to_all | solution.py:472
  156.5 17.3 %all-to-all-done.6 = f32[8,32,8,256]{3,2,1,0:T(8,128)S(1)} async-done(((f32[8,32,8,256]{3,2,1,0:T(8,128)}), f32[8,32,8,256]{3,2,1,0:T(8,128)S(1)}, u32[]{:S(2)}, u32[]{:S(2)}) %all-to-all-start.6) | async-done | bytes 2097184 | tf_op jit(solution)/shard_map/all_to_all | solution.py:472
  173.7 30.9 %all_to_all.82 = f32[8,32,8,256]{3,2,1,0:T(8,128)} all-to-all(f32[8,32,8,256]{3,2,1,0:T(8,128)} %get-tuple-element.45), channel_id=1, replica_groups=mesh['tm'=4,'line'=4,'core'=2] {'tm','core'}, dimensions={0} | all-to-all | bytes 4194304 | tf_op jit(solution)/shard_map/all_to_all | solution.py:472
  211.7 14.6 %relax.4 = (f32[4,64,8,256]{3,2,1,0:T(8,128)}, f32[4,64,8,256]{3,2,1,0:T(8,128)}, f32[2,4,8,8,256]{4,3,2,1,0:T(8,128)}) custom-call(s32[1]{0:T(128)} %bitcast.r_0_, f32[29,32,256]{2,1,0:T(8,128)} %coefs.1.r_0_.r_1_, f32[4,64,8,256]{3,2,1,0:T(8,128)} %bitcast.35, f32[4,64,8,256]{3,2,1,0:T(8,128)} %bitcast.49, f32[4,64,8,256]{3,2,1,0:T(8,128)} %bitcast.36, ...), custom_call_target="tpu_custom_call" | custom-call | tf_op jit(solution)/shard_map/relax/pallas_call | solution.py:531
  232.2 14.6 %relax.5 = (f32[4,64,8,256]{3,2,1,0:T(8,128)}, f32[4,64,8,256]{3,2,1,0:T(8,128)}, f32[2,4,8,8,256]{4,3,2,1,0:T(8,128)}) custom-call(s32[1]{0:T(128)} %bitcast.r_0_, f32[29,32,256]{2,1,0:T(8,128)} %coefs.1.r_0_.r_1_, f32[4,64,8,256]{3,2,1,0:T(8,128)} %bitcast.38, f32[4,64,8,256]{3,2,1,0:T(8,128)} %bitcast.47, f32[4,64,8,256]{3,2,1,0:T(8,128)} %bitcast.39, ...), custom_call_target="tpu_custom_call" | custom-call | tf_op jit(solution)/shard_map/relax/pallas_call | solution.py:531
  256.5 30.9 %all_to_all.83 = f32[8,32,8,256]{3,2,1,0:T(8,128)} all-to-all(f32[8,32,8,256]{3,2,1,0:T(8,128)} %get-tuple-element.52), channel_id=1, replica_groups=mesh['tm'=4,'line'=4,'core'=2] {'tm','core'}, dimensions={0} | all-to-all | bytes 4194304 | tf_op jit(solution)/shard_map/all_to_all | solution.py:472
  294.4 14.6 %relax.6 = (f32[4,64,8,256]{3,2,1,0:T(8,128)}, f32[4,64,8,256]{3,2,1,0:T(8,128)}, f32[2,4,8,8,256]{4,3,2,1,0:T(8,128)}) custom-call(s32[1]{0:T(128)} %bitcast.r_0_, f32[29,32,256]{2,1,0:T(8,128)} %coefs.1.r_0_.r_1_, f32[4,64,8,256]{3,2,1,0:T(8,128)} %bitcast.44, f32[4,64,8,256]{3,2,1,0:T(8,128)} %bitcast.51, f32[4,64,8,256]{3,2,1,0:T(8,128)} %bitcast.45, ...), custom_call_target="tpu_custom_call" | custom-call | tf_op jit(solution)/shard_map/relax/pallas_call | solution.py:531
  319.6 17.6 %all-gather.2 = f32[8,3,8,256]{3,2,1,0:T(8,128)} all-gather(f32[2,3,8,256]{3,2,1,0:T(8,128)} %get-tuple-element.36), channel_id=4, replica_groups=mesh['tm'=4,'line'=4,'core'=2] {'line'}, dimensions={0}, use_global_device_ids=true | all-gather | bytes 245760 | tf_op jit(solution)/shard_map/all_gather | solution.py:475
  357.4 16.7 %all-gather.5 = f32[8,3,8,256]{3,2,1,0:T(8,128)} all-gather(f32[2,3,8,256]{3,2,1,0:T(8,128)} %get-tuple-element.43), channel_id=7, replica_groups=mesh['tm'=4,'line'=4,'core'=2] {'line'}, dimensions={0}, use_global_device_ids=true | all-gather | bytes 245760 | tf_op jit(solution)/shard_map/all_gather | solution.py:475
  385.4 14.6 %relax.7 = (f32[4,64,8,256]{3,2,1,0:T(8,128)}, f32[4,64,8,256]{3,2,1,0:T(8,128)}, f32[2,4,8,8,256]{4,3,2,1,0:T(8,128)}) custom-call(s32[1]{0:T(128)} %bitcast.r_0_, f32[29,32,256]{2,1,0:T(8,128)} %coefs.1.r_0_.r_1_, f32[4,64,8,256]{3,2,1,0:T(8,128)} %bitcast.41, f32[4,64,8,256]{3,2,1,0:T(8,128)} %bitcast.53, f32[4,64,8,256]{3,2,1,0:T(8,128)} %bitcast.42, ...), custom_call_target="tpu_custom_call" | custom-call | tf_op jit(solution)/shard_map/relax/pallas_call | solution.py:531
  400.0 31.5 %all-gather.31.cloned.1.call-done = f32[8,4,8,8,256]{4,3,2,1,0:T(8,128)} async-done(((f32[2,4,8,8,256]{4,3,2,1,0:T(8,128)}), f32[8,4,8,8,256]{4,3,2,1,0:T(8,128)}) %all-gather.31.cloned.1.call-update) | async-done | bytes 2097168 | tf_op jit(solution)/shard_map/all_gather | solution.py:475
  442.2 16.3 %all-gather.8 = f32[8,3,8,256]{3,2,1,0:T(8,128)} all-gather(f32[2,3,8,256]{3,2,1,0:T(8,128)} %get-tuple-element.50), channel_id=10, replica_groups=mesh['tm'=4,'line'=4,'core'=2] {'line'}, dimensions={0}, use_global_device_ids=true | all-gather | bytes 245760 | tf_op jit(solution)/shard_map/all_gather | solution.py:475
  466.7 14.1 %all-gather.35.cloned.1.call-done = f32[8,4,8,8,256]{4,3,2,1,0:T(8,128)} async-done(((f32[2,4,8,8,256]{4,3,2,1,0:T(8,128)}), f32[8,4,8,8,256]{4,3,2,1,0:T(8,128)}) %all-gather.35.cloned.1.call-update) | async-done | bytes 2097168 | tf_op jit(solution)/shard_map/all_gather | solution.py:475
  491.5 14.6 %all-gather.11 = f32[8,3,8,256]{3,2,1,0:T(8,128)} all-gather(f32[2,3,8,256]{3,2,1,0:T(8,128)} %get-tuple-element.57), channel_id=13, replica_groups=mesh['tm'=4,'line'=4,'core'=2] {'line'}, dimensions={0}, use_global_device_ids=true | all-gather | bytes 245760 | tf_op jit(solution)/shard_map/all_gather | solution.py:475
  510.0 29.4 %all_to_all.84.refs_3_ = f32[8,32,8,256]{3,2,1,0:T(8,128)} all-to-all(f32[8,32,8,256]{3,2,1,0:T(8,128)} %bitcast.64), channel_id=1, replica_groups=mesh['tm'=4,'line'=4,'core'=2] {'tm','core'}, dimensions={0} | all-to-all | bytes 4194304 | tf_op jit(solution)/shard_map/all_to_all | solution.py:472
  539.3 29.9 %all_to_all.85.refs_0_ = f32[8,32,8,256]{3,2,1,0:T(8,128)} all-to-all(f32[8,32,8,256]{3,2,1,0:T(8,128)S(1)} %bitcast.58), channel_id=1, replica_groups=mesh['tm'=4,'line'=4,'core'=2] {'tm','core'}, dimensions={0} | all-to-all | bytes 4194304 | tf_op jit(solution)/shard_map/all_to_all | solution.py:472
  569.2 29.9 %all_to_all.86.refs_1_ = f32[8,32,8,256]{3,2,1,0:T(8,128)} all-to-all(f32[8,32,8,256]{3,2,1,0:T(8,128)S(1)} %bitcast.59), channel_id=1, replica_groups=mesh['tm'=4,'line'=4,'core'=2] {'tm','core'}, dimensions={0} | all-to-all | bytes 4194304 | tf_op jit(solution)/shard_map/all_to_all | solution.py:472
  599.1 29.7 %all_to_all.87.refs_2_ = f32[8,32,8,256]{3,2,1,0:T(8,128)} all-to-all(f32[8,32,8,256]{3,2,1,0:T(8,128)S(1)} %bitcast.61), channel_id=1, replica_groups=mesh['tm'=4,'line'=4,'core'=2] {'tm','core'}, dimensions={0} | all-to-all | bytes 4194304 | tf_op jit(solution)/shard_map/all_to_all | solution.py:472
  634.7 13.4 %inverse.2 = f32[32,256,256]{2,1,0:T(8,128)} custom-call(f32[8,32,8,256]{3,2,1,0:T(8,128)} %copy-done.7, f32[8,32,8,256]{3,2,1,0:T(8,128)} %all-to-all-done.5.refs_1_, f32[8,32,8,256]{3,2,1,0:T(8,128)} %copy-done.8, f32[8,32,8,256]{3,2,1,0:T(8,128)} %all_to_all.84.refs_3_, bf16[256,256]{1,0:T(8,128)(2,1)} %get-tuple-element.58.r_1_.r_3_.refs_4_, ...), custom_call_target="tpu_custom_call" | custom-call | tf_op jit(solution)/shard_map/inverse/pallas_call | solution.py:461
  660.4 13.4 %inverse.3 = f32[32,256,256]{2,1,0:T(8,128)} custom-call(f32[8,32,8,256]{3,2,1,0:T(8,128)} %all_to_all.85.refs_0_, f32[8,32,8,256]{3,2,1,0:T(8,128)} %all_to_all.86.refs_1_, f32[8,32,8,256]{3,2,1,0:T(8,128)} %all_to_all.87.refs_2_, f32[8,32,8,256]{3,2,1,0:T(8,128)} %copy-done.9, bf16[256,256]{1,0:T(8,128)(2,1)} %get-tuple-element.58.r_1_.r_3_.refs_4_, ...), custom_call_target="tpu_custom_call" | custom-call | tf_op jit(solution)/shard_map/inverse/pallas_call | solution.py:461
  (75 shorter events, 171.0 us)
Async XLA Ops:
  22.7 28.5 %all-to-all-start = ((f32[8,32,8,256]{3,2,1,0:T(8,128)}), f32[8,32,8,256]{3,2,1,0:T(8,128)S(1)}, u32[]{:S(2)}, u32[]{:S(2)}) async-start(f32[8,32,8,256]{3,2,1,0:T(8,128)} %get-tuple-element.30), calls=%async_computation | async-start | bytes 4194304 | tf_op jit(solution)/shard_map/all_to_all | solution.py:472
  51.1 31.1 %copy-start = (f32[8,32,8,256]{3,2,1,0:T(8,128)}, f32[8,32,8,256]{3,2,1,0:T(8,128)S(1)}, u32[]{:S(2)}) copy-start(f32[8,32,8,256]{3,2,1,0:T(8,128)S(1)} %all-to-all-done) | copy-start | bytes 6291460
  51.2 31.1 %copy-start.10 = (f32[8,32,8,256]{3,2,1,0:T(8,128)S(1)}, f32[8,32,8,256]{3,2,1,0:T(8,128)}, u32[]{:S(2)}) copy-start(f32[8,32,8,256]{3,2,1,0:T(8,128)} %get-tuple-element.37) | copy-start | bytes 6291460
  112.0 30.2 %all-to-all-start.4 = ((f32[8,32,8,256]{3,2,1,0:T(8,128)}), f32[8,32,8,256]{3,2,1,0:T(8,128)S(1)}, u32[]{:S(2)}, u32[]{:S(2)}) async-start(f32[8,32,8,256]{3,2,1,0:T(8,128)} %get-tuple-element.38), calls=%async_computation.4 | async-start | bytes 4194304 | tf_op jit(solution)/shard_map/all_to_all | solution.py:472
  117.9 93.8 %all-gather.21.cloned.1.call-start = ((), (), s32[]{:S(2)}) async-start(), calls=%async_computation.16 | async-start | bytes 1966080 | tf_op jit(solution)/shard_map/all_gather | solution.py:475
  143.6 30.2 %all-to-all-start.6 = ((f32[8,32,8,256]{3,2,1,0:T(8,128)}), f32[8,32,8,256]{3,2,1,0:T(8,128)S(1)}, u32[]{:S(2)}, u32[]{:S(2)}) async-start(f32[8,32,8,256]{3,2,1,0:T(8,128)} %get-tuple-element.44), calls=%async_computation.6 | async-start | bytes 4194304 | tf_op jit(solution)/shard_map/all_to_all | solution.py:472
  149.5 82.8 %all-gather.25.cloned.1.call-start = ((), (), s32[]{:S(2)}) async-start(), calls=%async_computation.18 | async-start | bytes 1966080 | tf_op jit(solution)/shard_map/all_gather | solution.py:475
  156.4 137.9 %all-gather.29.cloned.1.call-start = ((), (), s32[]{:S(2)}) async-start(), calls=%async_computation.20 | async-start | bytes 1966080 | tf_op jit(solution)/shard_map/all_gather | solution.py:475
  173.7 30.9 %copy-start.2 = (f32[8,32,8,256]{3,2,1,0:T(8,128)}, f32[8,32,8,256]{3,2,1,0:T(8,128)S(1)}, u32[]{:S(2)}) copy-start(f32[8,32,8,256]{3,2,1,0:T(8,128)S(1)} %all-to-all-done.6) | copy-start | bytes 6291460
  211.6 97.4 %all-gather.23.cloned.1.call-start = ((), (), s32[]{:S(2)}) async-start(), calls=%async_computation.17 | async-start | bytes 2621440 | tf_op jit(solution)/shard_map/all_gather | solution.py:475
  226.3 30.2 %all-to-all-start.9 = ((f32[8,32,8,256]{3,2,1,0:T(8,128)}), f32[8,32,8,256]{3,2,1,0:T(8,128)S(1)}, u32[]{:S(2)}, u32[]{:S(2)}) async-start(f32[8,32,8,256]{3,2,1,0:T(8,128)} %get-tuple-element.51), calls=%async_computation.9 | async-start | bytes 4194304 | tf_op jit(solution)/shard_map/all_to_all | solution.py:472
  232.2 114.7 %all-gather.27.cloned.1.call-start = ((), (), s32[]{:S(2)}) async-start(), calls=%async_computation.19 | async-start | bytes 2621440 | tf_op jit(solution)/shard_map/all_gather | solution.py:475
  246.8 138.6 %all-gather.33.cloned.1.call-start = ((), (), s32[]{:S(2)}) async-start(), calls=%async_computation.22 | async-start | bytes 1966080 | tf_op jit(solution)/shard_map/all_gather | solution.py:475
  256.5 30.9 %copy-start.1 = (f32[8,32,8,256]{3,2,1,0:T(8,128)}, f32[8,32,8,256]{3,2,1,0:T(8,128)S(1)}, u32[]{:S(2)}) copy-start(f32[8,32,8,256]{3,2,1,0:T(8,128)S(1)} %all-to-all-done.9) | copy-start | bytes 6291460
  294.3 137.3 %all-gather.31.cloned.1.call-start = ((), (), s32[]{:S(2)}) async-start(), calls=%async_computation.21 | async-start | bytes 2621440 | tf_op jit(solution)/shard_map/all_gather | solution.py:475
  341.1 37.0 %all-to-all-start.2 = ((f32[8,32,8,256]{3,2,1,0:T(8,128)}), f32[8,32,8,256]{3,2,1,0:T(8,128)S(1)}, u32[]{:S(2)}, u32[]{:S(2)}) async-start(f32[8,32,8,256]{3,2,1,0:T(8,128)} %bitcast.63), calls=%async_computation.2 | async-start | bytes 4194304 | tf_op jit(solution)/shard_map/all_to_all | solution.py:472
  379.4 83.0 %all-to-all-start.5 = ((f32[8,32,8,256]{3,2,1,0:T(8,128)}), f32[8,32,8,256]{3,2,1,0:T(8,128)}, u32[]{:S(2)}, u32[]{:S(2)}) async-start(f32[8,32,8,256]{3,2,1,0:T(8,128)} %bitcast.60), calls=%async_computation.5 | async-start | bytes 4194304 | tf_op jit(solution)/shard_map/all_to_all | solution.py:472
  383.9 96.9 %all-gather.35.cloned.1.call-start = ((), (), s32[]{:S(2)}) async-start(), calls=%async_computation.23 | async-start | bytes 2621440 | tf_op jit(solution)/shard_map/all_gather | solution.py:475
  462.5 47.5 %all-to-all-start.8 = ((f32[8,32,8,256]{3,2,1,0:T(8,128)}), f32[8,32,8,256]{3,2,1,0:T(8,128)S(1)}, u32[]{:S(2)}, u32[]{:S(2)}) async-start(f32[8,32,8,256]{3,2,1,0:T(8,128)} %bitcast.62), calls=%async_computation.8 | async-start | bytes 4194304 | tf_op jit(solution)/shard_map/all_to_all | solution.py:472
  510.0 29.4 %copy-start.8 = (f32[8,32,8,256]{3,2,1,0:T(8,128)}, f32[8,32,8,256]{3,2,1,0:T(8,128)S(1)}, u32[]{:S(2)}) copy-start(f32[8,32,8,256]{3,2,1,0:T(8,128)S(1)} %all-to-all-done.8.refs_2_) | copy-start | bytes 6291460
  510.0 29.4 %copy-start.4 = (f32[4,64,8,256]{3,2,1,0:T(8,128)S(1)}, f32[4,64,8,256]{3,2,1,0:T(8,128)}, u32[]{:S(2)}) copy-start(f32[4,64,8,256]{3,2,1,0:T(8,128)} %get-tuple-element.35.r_3_) | copy-start | bytes 6291460
  539.3 29.9 %copy-start.5 = (f32[4,64,8,256]{3,2,1,0:T(8,128)S(1)}, f32[4,64,8,256]{3,2,1,0:T(8,128)}, u32[]{:S(2)}) copy-start(f32[4,64,8,256]{3,2,1,0:T(8,128)} %get-tuple-element.42.r_3_) | copy-start | bytes 6291460
  569.2 29.9 %copy-start.6 = (f32[4,64,8,256]{3,2,1,0:T(8,128)S(1)}, f32[4,64,8,256]{3,2,1,0:T(8,128)}, u32[]{:S(2)}) copy-start(f32[4,64,8,256]{3,2,1,0:T(8,128)} %get-tuple-element.49.r_3_) | copy-start | bytes 6291460
  628.8 30.2 %all-to-all-start.15 = ((f32[8,32,8,256]{3,2,1,0:T(8,128)}), f32[8,32,8,256]{3,2,1,0:T(8,128)S(1)}, u32[]{:S(2)}, u32[]{:S(2)}) async-start(f32[8,32,8,256]{3,2,1,0:T(8,128)} %bitcast.32), calls=%async_computation.15 | async-start | bytes 4194304 | tf_op jit(solution)/shard_map/all_to_all | solution.py:472
  (3 other events, 4.1 us)
Sparse Core Ops, SparseCore 0:
  131.1 38.1 all-gather.20
  170.9 35.8 all-gather.24
  211.7 38.1 all-gather.28
  251.4 44.5 all-gather.22
  297.4 47.6 all-gather.26
  346.4 38.9 all-gather.32
  387.0 44.5 all-gather.30
  433.1 47.6 all-gather.34
